TPU v7x, 256 devices: a 4x2x16 block of a 4x16x16 slice. The times are simulated.
256 devices in a mesh: groups: 2 (over y), ep: 128 (over x, z, core).
Axes of the slice: x: 4, y: 2, z: 16, core: 2. Of those that a mesh axis runs over, the one named last changes fastest.
The devices are a block of a 4x16x16 slice.
Arguments:
- tokens: bfloat16 [32768, 1440], P(('groups', 'ep')), parts along dimension 0, may hold values from -6 to 6
- expert_ids: int32 [32768, 4], P(('groups', 'ep')), parts along dimension 0, may hold values from 0 to 127, as said below
- combine: float32 [32768, 4], P(('groups', 'ep')), parts along dimension 0, may hold values from 0.05 to 1
- gate_weight: bfloat16 [128, 1440, 1440], P('ep'), may hold values from -0.15625 to 0.15625
- up_weight: bfloat16 [128, 1440, 1440], P('ep'), may hold values from -0.15625 to 0.15625
- down_weight: bfloat16 [128, 1440, 1440], P('ep'), may hold values from -0.15625 to 0.15625
Outputs:
- mixture: bfloat16 [32768, 1440], P(('groups', 'ep')), parts along dimension 0
There are 2 independent parts, one for each index of `groups`. A program takes and returns all parts, laid end to end along the dimension named above; an argument that names none is the same for every part. Nothing has to cross between parts.
Inputs may be any that keep to these rules, and one draw needn't show every extreme that they name: `expert_ids`: each row names 4 different experts. In the rows of one device (aligned blocks of 128 rows) no expert is named more than 8 times, and some expert is named exactly 8 times in every block.
All inputs are finite; a program needn't handle non-finite values.
Results may differ from a plain program's by a relative error of at most 0.0058.
Values may be sent and summed in bfloat16 or wider, within the bound.
A program may use at most 64 MiB of HBM per device.

v0:
```python
import jax
import jax.numpy as jnp
from jax import lax
from jax.sharding import PartitionSpec as P

alpha_gate = 1.702


def run_expert_block(row_block, gate_proj, up_proj, down_proj):
    gate_part = jnp.dot(row_block, gate_proj, preferred_element_type=jnp.float32)
    up_part = jnp.dot(row_block, up_proj, preferred_element_type=jnp.float32)
    hidden = ((up_part + 1.0) * gate_part * jax.nn.sigmoid(alpha_gate * gate_part)).astype(
        jnp.bfloat16
    )
    return jnp.dot(hidden, down_proj, preferred_element_type=jnp.float32).astype(jnp.bfloat16)


def on_device(tokens, expert_ids, combine, gate_weight, up_weight, down_weight):
    members = lax.axis_size("ep")
    tokens_here, fanout = expert_ids.shape
    features = tokens.shape[1]
    capacity = 2 * tokens_here * fanout // members
    received_rows = members * capacity
    flat_ids = expert_ids.reshape(-1)
    onehot = (flat_ids[:, None] == jnp.arange(members, dtype=jnp.int32)[None, :]).astype(jnp.int32)
    running = jnp.cumsum(onehot, axis=0) - onehot
    slot_rank = jnp.sum(running * onehot, axis=1)
    target = flat_ids * capacity + slot_rank
    source_token = jnp.arange(tokens_here * fanout, dtype=jnp.int32) // fanout
    outgoing = (
        jnp.zeros((received_rows, features), jnp.bfloat16).at[target].set(tokens[source_token])
    )
    outgoing = outgoing.reshape(members, capacity, features)
    gate_proj, up_proj, down_proj = (gate_weight[0], up_weight[0], down_weight[0])
    arrived = lax.all_to_all(outgoing, "ep", split_axis=0, concat_axis=0, tiled=True)
    shape_here = arrived.shape
    answers = run_expert_block(
        arrived.reshape(-1, features), gate_proj, up_proj, down_proj
    ).reshape(shape_here)
    returned = lax.all_to_all(answers, "ep", split_axis=0, concat_axis=0, tiled=True)
    selected_experts = (
        returned.reshape(-1, features)[target]
        .astype(jnp.float32)
        .reshape(tokens_here, fanout, features)
    )
    mixture = jnp.sum(selected_experts * combine[:, :, None], axis=1)
    return mixture.astype(jnp.bfloat16)


def solution(mesh):
    in_specs = (
        P(("groups", "ep"), None),
        P(("groups", "ep"), None),
        P(("groups", "ep"), None),
        P("ep", None, None),
        P("ep", None, None),
        P("ep", None, None),
    )
    out_specs = P(("groups", "ep"), None)
    return jax.shard_map(
        on_device, mesh=mesh, in_specs=in_specs, out_specs=out_specs, check_vma=False
    )
```

profile of v0, /device:TPU:40, one launch (start us, length us, event | category | flops | bytes accessed | tf_op | source)
XLA Modules:
  0.0 377.3 jit_solution(830638386292658426)
XLA Ops:
  0.0 0.8 copy.28
  0.8 0.1 eq.29
  0.9 0.1 eq.25
  1.0 0.7 broadcast_multiply_fusion
  1.7 0.1 copy.30
  1.8 0.2 fusion.25
  2.1 0.1 copy.27
  2.2 0.1 mul.41
  2.4 1.2 copy.32
  3.5 0.2 fusion.24
  3.8 9.2 %scatter_custom_fusion = bf16[1024,1440]{1,0:T(8,128)(2,1)S(1)} fusion(s32[512]{0:T(512)S(1)} %bitcast.49, bf16[128,1440]{1,0:T(8,128)(2,1)S(1)} %copy.32, s32[1024]{0:T(1024)S(1)} %pad_clamp_fusion.1, bf16[]{:T(256)} %constant.26.clone.1), kind=kCustom, calls=%fused_computation.16 | custom fusion | bytes 2949122 | tf_op jit(solution)/shard_map/scatter | solution.py:31
  12.9 0.0 copy-start.2
  13.0 172.0 %all_to_all.10 = bf16[128,8,1440]{2,1,0:T(8,128)(2,1)S(1)} all-to-all(bf16[128,8,1440]{2,1,0:T(8,128)(2,1)S(1)} %bitcast.44), channel_id=1, replica_groups=mesh['groups'=2,'ep'=128] {'ep'}, dimensions={0} | all-to-all | bytes 5898240 | tf_op jit(solution)/shard_map/all_to_all | solution.py:35
  185.0 0.0 copy-start
  185.0 1.7 copy-done
  186.7 0.0 copy-done.2
  186.7 6.7 %fusion.8 = f32[1024,1440]{0,1:T(8,128)} fusion(bf16[1,1440,1440]{2,1,0:T(8,128)(2,1)S(1)} %copy-done.2, bf16[128,8,1440]{2,1,0:T(8,128)(2,1)S(1)} %all_to_all.10), kind=kOutput, calls=%fused_computation.8 | convolution fusion | flops 4246732800 | bytes 12994560 | tf_op jit(solution)/shard_map/dot_general | solution.py:11
  193.4 17.1 %fusion.10 = bf16[1024,1440]{0,1:T(8,128)(2,1)S(1)} fusion(bf16[1,1440,1440]{2,1,0:T(8,128)(2,1)} %param.11, f32[1024,1440]{0,1:T(8,128)} %fusion.8, bf16[1,1440,1440]{2,1,0:T(8,128)(2,1)} %param.9, bf16[128,8,1440]{2,1,0:T(8,128)(2,1)} %copy-done), kind=kOutput, calls=%fused_computation.10 | convolution fusion | flops 8506736640 | bytes 20090880 | tf_op jit(solution)/shard_map/dot_general | solution.py:15
  210.5 2.9 copy.33
  213.4 0.0 copy-start.1
  213.4 14.1 %all-to-all-start.1 = ((bf16[128,8,1440]{2,1,0:T(8,128)(2,1)}), bf16[128,8,1440]{2,1,0:T(8,128)(2,1)S(1)}, u32[]{:S(2)}, u32[]{:S(2)}) async-start(bf16[128,8,1440]{2,1,0:T(8,128)(2,1)} %bitcast.43), calls=%async_computation.1 | async-start | bytes 6291456 | tf_op jit(solution)/shard_map/all_to_all | solution.py:40
  227.6 0.0 copy-done.1
  227.6 0.7 copy.34
  228.3 139.1 %all-to-all-done.1 = bf16[128,8,1440]{2,1,0:T(8,128)(2,1)S(1)} async-done(((bf16[128,8,1440]{2,1,0:T(8,128)(2,1)}), bf16[128,8,1440]{2,1,0:T(8,128)(2,1)S(1)}, u32[]{:S(2)}, u32[]{:S(2)}) %all-to-all-start.1) | async-done | bytes 2949152 | tf_op jit(solution)/shard_map/all_to_all | solution.py:40
  367.4 3.0 gather_fusion
  370.4 2.9 reshape.111
  373.3 3.1 multiply_reduce_fusion
  376.4 0.9 copy.35
  (10 shorter events, 0.1 us)
Async XLA Ops:
  12.9 173.8 %copy-start.2 = (bf16[1,1440,1440]{2,1,0:T(8,128)(2,1)S(1)}, bf16[1,1440,1440]{2,1,0:T(8,128)(2,1)}, u32[]{:S(2)}) copy-start(bf16[1,1440,1440]{2,1,0:T(8,128)(2,1)} %param.10) | copy-start | bytes 12441604
  185.0 1.7 copy-start
  213.4 14.2 %copy-start.1 = (f32[128,4]{0,1:T(4,128)S(1)}, f32[128,4]{0,1:T(4,128)}, u32[]{:S(2)}) copy-start(f32[128,4]{0,1:T(4,128)} %param.8) | copy-start | bytes 6148
  213.4 154.0 %all-to-all-start.1 = ((bf16[128,8,1440]{2,1,0:T(8,128)(2,1)}), bf16[128,8,1440]{2,1,0:T(8,128)(2,1)S(1)}, u32[]{:S(2)}, u32[]{:S(2)}) async-start(bf16[128,8,1440]{2,1,0:T(8,128)(2,1)} %bitcast.43), calls=%async_computation.1 | async-start | bytes 6291456 | tf_op jit(solution)/shard_map/all_to_all | solution.py:40
where the time goes:
time: 378 us; the launch traced here: 377 us
  blocking collectives  172 us (46%)
  waiting for transfers between devices  139 us (37%)
  local copies, waits for them, and re-layouts  23.9 us (6%)
  matrix products  23.8 us (6%)
  starting transfers between devices  14.1 us (4%)
  other arithmetic  4.34 us (1%)
    all_to_all x1, blocking collectives, on_device(): lax.all_to_all(outgoing, 'ep', split_axis=0, concat_axis=0, tiled=True)  172 us
    all_to_all x1, waiting for transfers between devices, on_device(): lax.all_to_all(answers, 'ep', split_axis=0, concat_axis=0, tiled=True)  139 us
    dot_general x1, matrix products, run_expert_block(): jnp.dot(hidden, down_proj, preferred_element_type=jnp.float32)  17.1 us
    all_to_all x1, starting transfers between devices, on_device(): lax.all_to_all(answers, 'ep', split_axis=0, concat_axis=0, tiled=True)  14.1 us
    scatter x1, local copies, waits for them, and re-layouts, on_device(): jnp.zeros((received_rows, features), jnp.bfloat16).at[target]  9.15 us
  transfers between devices with their start and end apart: 1, of which 1 were waited for; matrix products, arithmetic and copies ran while one was open for 0% of the time, Pallas kernels for 0%

commit v1 on v0

v1 whole, which is shorter than its diff:
```python
import functools

import jax
import jax.numpy as jnp
from jax import lax
from jax.experimental import pallas as pl
from jax.experimental.pallas import tpu as pltpu
from jax.sharding import PartitionSpec as P

alpha_gate = 1.702
CHIPS_X = 4
CORES = 2
BF16 = jnp.bfloat16
F32 = jnp.float32
MESH = pl.DeviceIdType.MESH
LANES = 128


def log2(n):
    return n.bit_length() - 1


def layer_kernel(
    nx, nz, nc, cap, top, width,
    x_hbm, wg_hbm, wu_hbm, wd_hbm, o_ref,
    G, SEL, RECV, OUT, RET, PP, SW, CH, HID, wg, wu, wd,
    lsem, wsem, zs, zr, xs, xr, ys, yr, cs, cr,
):
    half = nz // 2
    plane = nx * nc
    tokens, padded = G.shape[2], G.shape[3]
    piece_rows = tokens // 2
    per = 2 * cap
    slots = plane * per
    meta_at = width - (padded - LANES)

    me = lax.axis_index("ep")
    core = lax.rem(me, nc)
    z = lax.rem(me // nc, nz)
    x = me // (nc * nz)
    seat = x * nc + core

    def device(x_, z_, c_):
        return {"ep": (x_ * nz + z_) * nc + c_}

    up = device(x, lax.rem(z + 1, nz), core)
    down = device(x, lax.rem(z + nz - 1, nz), core)
    ring = (up, down)
    seats = [lax.rem(seat + o, plane) for o in range(1, plane)]
    peers = [device(s // nc, z, lax.rem(s, nc)) for s in seats]

    loads = [
        pltpu.make_async_copy(
            x_hbm.at[pl.ds(i * piece_rows, piece_rows)],
            G.at[0, 0, pl.ds(i * piece_rows, piece_rows)],
            lsem.at[i],
        )
        for i in range(2)
    ]
    for load in loads:
        load.start()
    weight_loads = [
        pltpu.make_async_copy(src.at[0], dst, wsem.at[i])
        for i, (src, dst) in enumerate(((wg_hbm, wg), (wu_hbm, wu), (wd_hbm, wd)))
    ]
    for load in weight_loads:
        load.start()

    barrier = pltpu.get_barrier_semaphore()
    for peer in (*ring, *peers):
        pl.semaphore_signal(barrier, inc=1, device_id=peer, device_id_type=MESH)
    pl.semaphore_wait(barrier, len(ring) + len(peers))

    def hop(t, d, piece, last=False):
        rows = pl.ds(piece * piece_rows, piece_rows)
        src = G.at[t - 1, d, rows] if not isinstance(t, int) or t > 1 else G.at[0, 0, rows]
        dst = G.at[0, 1, rows] if last else G.at[t, d, rows]
        return pltpu.make_async_remote_copy(
            src_ref=src, dst_ref=dst, send_sem=zs.at[t, d, piece], recv_sem=zr.at[t, d, piece],
            device_id=ring[d], device_id_type=MESH,
        )

    def fan(src, dst, send, recv, p, i):
        at = pl.multiple_of(seats[i] * per, per)
        to = pl.multiple_of(seat * per, per)
        return pltpu.make_async_remote_copy(
            src_ref=src.at[p, pl.ds(at, per)], dst_ref=dst.at[p, pl.ds(to, per)],
            send_sem=send.at[p], recv_sem=recv.at[p], device_id=peers[i], device_id_type=MESH,
        )

    def fan_all(src, dst, send, recv, p):
        n = (plane - 1) * per
        return pltpu.make_async_remote_copy(
            src_ref=src.at[p, pl.ds(0, n)], dst_ref=dst.at[p, pl.ds(0, n)],
            send_sem=send.at[p], recv_sem=recv.at[p], device_id=peers[0], device_id_type=MESH,
        )

    def send_fan(src, dst, send, recv, p):
        for i in range(plane - 1):
            fan(src, dst, send, recv, p, i).start()
        mine = pl.ds(pl.multiple_of(seat * per, per), per)
        dst[p, mine] = src[p, mine]

    def select(p):
        lane = lax.broadcasted_iota(jnp.int32, (tokens, slots), 1)
        j = lane >> log2(per)
        side = (lane >> log2(cap)) & 1
        place = (lane & (cap - 1)).astype(F32)
        expert = (((j >> log2(nc)) * nz + z) * nc + (j & (nc - 1))).astype(F32)
        row = lax.broadcasted_iota(jnp.int32, (tokens, tokens), 0)
        col = lax.broadcasted_iota(jnp.int32, (tokens, tokens), 1)
        before = jnp.where(col < row, 1.0, 0.0).astype(BF16)
        picks = []
        for d in range(2):
            meta = G[p, d, :, padded - LANES :].astype(F32)
            on_side = jnp.where(side == d, expert, -1.0)
            hit = jnp.zeros((tokens, slots), F32)
            high = jnp.zeros((tokens, slots), F32)
            low = jnp.zeros((tokens, slots), F32)
            for k in range(top):
                at = meta_at + k
                same = meta[:, at : at + 1] == on_side
                hit = jnp.where(same, 1.0, hit)
                high = jnp.where(same, meta[:, at + top : at + top + 1], high)
                low = jnp.where(same, meta[:, at + 2 * top : at + 2 * top + 1], low)
            rank = jnp.dot(before, hit.astype(BF16), preferred_element_type=F32)
            keep = rank == place
            picks.append(jnp.where(keep, hit, 0.0).astype(BF16))
            SW[p, 0, d] = jnp.where(keep, high, 0.0).astype(BF16)
            SW[p, 1, d] = jnp.where(keep, low, 0.0).astype(BF16)
        pick = jnp.concatenate(picks, axis=0)
        blocks = jnp.concatenate([G[p, 0], G[p, 1]], axis=0)
        chosen = lax.dot_general(
            pick, blocks, (((0,), (0,)), ((), ())), preferred_element_type=F32
        )
        SEL[p] = chosen.astype(BF16)
        send_fan(SEL, RECV, xs, xr, p)

    def expert_in(p):
        fan_all(SEL, RECV, xs, xr, p).wait_recv()
        rows = RECV[p, :, :width]
        gate = jnp.dot(rows, wg[...], preferred_element_type=F32)
        up_part = jnp.dot(rows, wu[...], preferred_element_type=F32)
        HID[...] = ((up_part + 1.0) * gate * jax.nn.sigmoid(alpha_gate * gate)).astype(BF16)

    def expert_out(p):
        OUT[p, :, :width] = jnp.dot(HID[...], wd[...], preferred_element_type=F32).astype(BF16)
        send_fan(OUT, RET, ys, yr, p)

    def mix(p):
        fan_all(OUT, RET, ys, yr, p).wait_recv()
        answers = RET[p]
        for d in range(2):
            PP[p, d] = jnp.dot(SW[p, 0, d], answers, preferred_element_type=F32) + jnp.dot(
                SW[p, 1, d], answers, preferred_element_type=F32
            )

    for piece in range(2):
        loads[piece].wait()
        for d in range(2):
            hop(1, d, piece).start()

    def step(t, unused):
        @pl.when((t >= 1) & (t < half))
        def _():
            for d in range(2):
                hop(t, d, 1).wait_recv()

            @pl.when(t < half - 1)
            def _():
                for d in range(2):
                    hop(t + 1, d, 1).start()

            @pl.when(t == half - 1)
            def _():
                hop(t + 1, 1, 1, last=True).start()

        @pl.when(t == half)
        def _():
            hop(t, 1, 1, last=True).wait_recv()

        @pl.when((t >= 1) & (t <= half))
        def _():
            select(lax.rem(t, half))

        @pl.when(t == 2)
        def _():
            for load in weight_loads:
                load.wait()

        @pl.when((t >= 2) & (t <= half + 1))
        def _():
            expert_in(lax.rem(t - 1, half))

        @pl.when(t + 1 < half)
        def _():
            for d in range(2):
                hop(t + 1, d, 0).wait_recv()

            @pl.when(t + 2 < half)
            def _():
                for d in range(2):
                    hop(t + 2, d, 0).start()

            @pl.when(t + 2 == half)
            def _():
                hop(t + 2, 0, 0, last=True).start()

        @pl.when(t + 1 == half)
        def _():
            hop(t + 1, 0, 0, last=True).wait_recv()

        @pl.when((t >= 2) & (t <= half + 1))
        def _():
            expert_out(lax.rem(t - 1, half))

        @pl.when(t >= 3)
        def _():
            mix(lax.rem(t - 2, half))

        return unused

    lax.fori_loop(0, half + 2, step, 0)

    for t in range(1, half + 1):
        for d in range(2):
            for piece in range(2):
                if t < half or piece == d:
                    hop(t, d, piece, last=t == half).wait_send()

    def link(s, d, piece):
        rows = pl.ds(piece * piece_rows, piece_rows)
        return pltpu.make_async_remote_copy(
            src_ref=G.at[s, d, rows] if s < half else G.at[0, 1, rows],
            dst_ref=CH.at[d, s - 1, rows],
            send_sem=cs.at[s, d, piece], recv_sem=cr.at[s - 1, d, piece],
            device_id=ring[1 - d], device_id_type=MESH,
        )

    def pass_on(s, d, piece):
        rows = pl.ds(piece * piece_rows, piece_rows)
        at = (s, d) if s < half else (0, 1)
        total = PP[(*at, rows)]
        if s < half - 1 or (s == half - 1 and piece == d):
            link(s + 1, d, piece).wait_recv()
            total = total + CH[d, s, rows].astype(F32)
        G[(*at, rows)] = total.astype(BF16)
        link(s, d, piece).start()

    for d in range(2):
        pass_on(half - 1, d, 1 - d)
    mix(0)
    for i in range(half):
        for d in range(2):
            pass_on(half - i, d, d)
        if half - 2 - i >= 1:
            for d in range(2):
                pass_on(half - 2 - i, d, 1 - d)

    for piece in (1, 0):
        rows = pl.ds(piece * piece_rows, piece_rows)
        total = PP[0, 0, rows]
        for d in range(2):
            link(1, d, piece).wait_recv()
            total = total + CH[d, 0, rows].astype(F32)
        o_ref[rows] = total[:, :width].astype(BF16)

    for s in range(1, half + 1):
        for d in range(2):
            for piece in range(2):
                if s < half or piece == d:
                    link(s, d, piece).wait_send()
    for p in range(half):
        fan_all(SEL, RECV, xs, xr, p).wait_send()
        fan_all(OUT, RET, ys, yr, p).wait_send()


def on_device(nx, nc, tokens, expert_ids, combine, gate_weight, up_weight, down_weight):
    members = lax.axis_size("ep")
    nz = members // (nx * nc)
    half = nz // 2
    rows, width = tokens.shape
    top = expert_ids.shape[1]
    hidden = gate_weight.shape[2]
    cap = 2 * rows * top // members
    slots = nx * nc * 2 * cap
    high = lax.reduce_precision(combine, 8, 7)
    low = combine - high
    padded = -(-(width + 3 * top) // LANES) * LANES
    packed = jnp.concatenate(
        [
            tokens,
            expert_ids.astype(BF16),
            high.astype(BF16),
            low.astype(BF16),
            jnp.zeros((rows, padded - width - 3 * top), BF16),
        ],
        axis=1,
    )
    dma = pltpu.SemaphoreType.DMA
    any_space = pl.BlockSpec(memory_space=pl.ANY)
    return pl.pallas_call(
        functools.partial(layer_kernel, nx, nz, nc, cap, top, width),
        out_shape=jax.ShapeDtypeStruct((rows, width), BF16),
        in_specs=[any_space] * 4,
        out_specs=pl.BlockSpec(memory_space=pltpu.VMEM),
        scratch_shapes=[
            pltpu.VMEM((half, 2, rows, padded), BF16),
            pltpu.VMEM((half, slots, padded), BF16),
            pltpu.VMEM((half, slots, padded), BF16),
            pltpu.VMEM((half, slots, padded), BF16),
            pltpu.VMEM((half, slots, padded), BF16),
            pltpu.VMEM((half, 2, rows, padded), F32),
            pltpu.VMEM((half, 2, 2, rows, slots), BF16),
            pltpu.VMEM((2, half, rows, padded), BF16),
            pltpu.VMEM((slots, hidden), BF16),
            pltpu.VMEM((width, hidden), BF16),
            pltpu.VMEM((width, hidden), BF16),
            pltpu.VMEM((hidden, width), BF16),
            dma((2,)),
            dma((3,)),
            dma((half + 1, 2, 2)),
            dma((half + 1, 2, 2)),
            dma((half,)),
            dma((half,)),
            dma((half,)),
            dma((half,)),
            dma((half + 1, 2, 2)),
            dma((half + 1, 2, 2)),
        ],
        compiler_params=pltpu.CompilerParams(
            collective_id=0, has_side_effects=True, vmem_limit_bytes=67_043_328
        ),
        name="layer",
    )(packed, gate_weight, up_weight, down_weight)


def solution(mesh, nx=CHIPS_X, nc=CORES):
    in_specs = (
        P(("groups", "ep"), None),
        P(("groups", "ep"), None),
        P(("groups", "ep"), None),
        P("ep", None, None),
        P("ep", None, None),
        P("ep", None, None),
    )
    out_specs = P(("groups", "ep"), None)
    return jax.shard_map(
        functools.partial(on_device, nx, nc),
        mesh=mesh, in_specs=in_specs, out_specs=out_specs, check_vma=False,
    )
```

time: 378 us -> 185 us (0.49)
  Pallas kernels: 0 us -> 178 us
  blocking collectives: 172 us -> 0 us
  waiting for transfers between devices: 139 us -> 0 us
  matrix products: 23.8 us -> 0 us
  local copies, waits for them, and re-layouts: 23.9 us -> 5.12 us
  starting transfers between devices: 14.1 us -> 0 us
    pallas_call x0 -> x1, Pallas kernels: none -> 178 us  [on_device(): pl.pallas_call(functools.partial(layer_kernel, nx, nz, nc, cap, top, widt...]
    all_to_all x1 -> x0, blocking collectives: 172 us -> none  [on_device(): lax.all_to_all(outgoing, 'ep', split_axis=0, concat_axis=0, tiled=True)]
    all_to_all x1 -> x0, waiting for transfers between devices: 139 us -> none  [on_device(): lax.all_to_all(answers, 'ep', split_axis=0, concat_axis=0, tiled=True)]
    dot_general x2 -> x0, matrix products: 23.8 us -> none  [the longest x1 17.1 us: run_expert_block(): jnp.dot(hidden, down_proj, preferred_element_type=jnp.float32)]
    all_to_all x1 -> x0, starting transfers between devices: 14.1 us -> none  [on_device(): lax.all_to_all(answers, 'ep', split_axis=0, concat_axis=0, tiled=True)]
    scatter x1 -> x0, local copies, waits for them, and re-layouts: 9.15 us -> none  [on_device(): jnp.zeros((received_rows, features), jnp.bfloat16).at[target]]
    convert_element_type x2, local copies, waits for them, and re-layouts: 5.85 us -> 0.27 us  [the longest x1 0.13 us: on_device(): expert_ids.astype(BF16)]
  transfers between devices with their start and end apart: 1 -> 0, of which waited for: 1 -> 0; matrix products, arithmetic and copies ran while one was open for 0% -> 0% of each run, Pallas kernels for 0% -> 0%
where the time goes in v1:
time: 185 us; the launch traced here: 184 us
  Pallas kernels  178 us (96%)
  local copies, waits for them, and re-layouts  5.12 us (3%)
    pallas_call x1, Pallas kernels, on_device(): pl.pallas_call(functools.partial(layer_kernel, nx, nz, nc, cap, top, widt...  178 us

profile of v1, /device:TPU:40, one launch (start us, length us, event | category | flops | bytes accessed | tf_op | source)
XLA Modules:
  0.0 184.4 jit_solution(3141537958473358698)
XLA Ops:
  0.0 0.7 convert_element_type.9
  0.7 0.7 fusion
  1.4 0.1 copy.15
  1.5 0.1 copy.16
  1.6 0.1 copy.13
  1.8 0.8 copy.12
  2.6 1.2 copy.14
  3.7 0.9 concatenate.3.x_hbm
  4.6 177.9 %layer.1 = bf16[128,1440]{1,0:T(8,128)(2,1)} custom-call(bf16[128,1536]{1,0:T(8,128)(2,1)} %concatenate.3.x_hbm, bf16[1,1440,1440]{2,1,0:T(8,128)(2,1)} %wg_hbm.1, bf16[1,1440,1440]{2,1,0:T(8,128)(2,1)} %wu_hbm.1, bf16[1,1440,1440]{2,1,0:T(8,128)(2,1)} %wd_hbm.1), custom_call_target="tpu_custom_call" | custom-call | tf_op jit(solution)/shard_map/layer/pallas_call | solution.py:302
  182.5 1.9 %copy.17 = bf16[128,1440]{0,1:T(8,128)(2,1)} copy(bf16[128,1440]{1,0:T(8,128)(2,1)} %layer.1) | data formatting | bytes 737280 | tf_op jit(solution)/shard_map/layer/pallas_call | solution.py:302
  (2 shorter events, 0.0 us)
